TPU v7x, 128 devices: a whole 4x4x4 slice. The times are simulated.
128 devices in a mesh: row: 8 (over z, core), col: 16 (over y, x).
Axes of the slice: x: 4, y: 4, z: 4, core: 2. Of those that a mesh axis runs over, the one named last changes fastest.
Arguments:
- ainv_anc: bfloat16 [24576, 24576], P('row', 'col'), may hold values from -6 to 6
- l_panel: bfloat16 [1536, 24576], P('col', 'row'), may hold values from -0.078125 to 0.078125
- diag_inv: float32 [1536, 768], P('col', 'row'), may hold values from -6 to 6
- struct_mask: int32 [2, 192], replicated, may hold values 0 or 1
- pieces: float32 [24576, 32, 128], P(('row', 'col')), may hold values from -6 to 6
- tile_owner: int32 [24576, 1], P(('row', 'col')), may hold values from 0 to 127; in each aligned block of 192 rows (0 to 191, 192 to 383, ...) at most 3 rows name the same one
Outputs:
- ainv_upper: bfloat16 [1536, 24576], P('col', 'row')
- ainv_diag: float32 [1536, 768], P('col', 'row')
- moved: float32 [49152, 32, 128], P(('row', 'col'))
Inputs may be any that keep to these rules, and one draw needn't show every extreme that they name: `tile_owner`: among the 192 pieces of one device no owner is named more than 3 times, a bound that some block reaches.
All inputs are finite; a program needn't handle non-finite values.
Results may differ from a plain program's by a relative error of at most 0.015.
Values may be sent and summed in bfloat16 or wider, within the bound.
A program may use at most 128 MiB of HBM per device.

v0:
```python
import jax
import jax.numpy as jnp
from jax import lax
from jax.sharding import PartitionSpec as P

W = 768
AB = 128
SLOT = 3


def broadcast(value, axis, root):
    mine = lax.axis_index(axis) == root
    return lax.psum(jnp.where(mine, value, jnp.zeros_like(value)), axis)


def cut_along(value, dim, count):
    before, after = (value.shape[:dim], value.shape[dim + 1 :])
    return jnp.moveaxis(value.reshape(*before, count, -1, *after), dim, 0)


def sum_at_owner(value, axis, dim):
    parts = cut_along(value, dim, lax.axis_size(axis))
    arrived = lax.all_to_all(parts, axis, split_axis=0, concat_axis=0, tiled=True)
    return arrived.astype(jnp.float32).sum(axis=0)


def joined_along(parts, dim):
    shape = list(parts.shape[1:])
    shape[dim] *= parts.shape[0]
    return jnp.moveaxis(parts, 0, dim).reshape(shape)


def joined_exchange(value, axis, axes, splits, concats):
    sizes = [lax.axis_size(a) for a in axes]
    parts = cut_along(value, splits[0], sizes[0])
    parts = jnp.moveaxis(cut_along(parts, splits[1] + 1, sizes[1]), 0, 1)
    inside = parts.shape[2:]
    parts = parts.reshape(-1, *inside)
    parts = lax.all_to_all(parts, axis, split_axis=0, concat_axis=0, tiled=True)
    parts = joined_along(parts.reshape(*sizes, *inside), concats[0] + 1)
    return joined_along(parts, concats[1])


def local(ainv_anc, l_panel, diag_inv, struct_mask, pieces, tile_owner):
    row_devices = lax.axis_size("row")
    col_devices = lax.axis_size("col")
    row_index = lax.axis_index("row")
    col_index = lax.axis_index("col")
    slab_rows = l_panel.shape[0]
    local_rows = l_panel.shape[1]
    cross_width = ainv_anc.shape[1]
    group_ratio = col_devices // row_devices
    supernode = col_index * slab_rows // W
    block_count = local_rows // AB
    keep_blocks = lax.dynamic_slice(
        struct_mask, (supernode, row_index * block_count), (1, block_count)
    )
    keep_rows = (
        jnp.broadcast_to(keep_blocks[:, :, None], (1, block_count, AB)).reshape(1, local_rows) > 0
    )
    masked = jnp.where(keep_rows, l_panel, jnp.zeros_like(l_panel))
    gathered = lax.all_gather(masked, "col", axis=0, tiled=True)
    offset = col_index % group_ratio * cross_width
    own_cross = lax.dynamic_slice_in_dim(gathered, offset, cross_width, 1)
    cross_rows = broadcast(own_cross, "row", col_index // group_ratio)
    product = lax.psum_scatter(
        lax.dot_general(
            cross_rows, ainv_anc, (((1,), (1,)), ((), ())), preferred_element_type=jnp.float32
        ).astype(jnp.bfloat16),
        "col",
        scatter_dimension=0,
        tiled=True,
    ).astype(jnp.float32)
    upper_rows = jnp.where(keep_rows, -product, jnp.zeros_like(product)).astype(jnp.bfloat16)
    own_block = lax.dynamic_slice_in_dim(gathered, supernode * W, W, 0)
    diag_part = lax.dot_general(
        upper_rows, own_block, (((1,), (1,)), ((), ())), preferred_element_type=jnp.float32
    )
    summed = sum_at_owner(diag_part.astype(jnp.bfloat16), "row", 1)
    ainv_diag = diag_inv - summed
    devices_all = row_devices * col_devices
    owners = tile_owner[:, 0]
    onehot = (owners[:, None] == jnp.arange(devices_all, dtype=jnp.int32)[None, :]).astype(
        jnp.int32
    )
    earlier = jnp.cumsum(onehot, axis=0) - onehot
    rank_in_dest = jnp.sum(earlier * onehot, axis=1)
    slot_index = owners * SLOT + rank_in_dest
    piece_rows = pieces.shape[1]
    piece_cols = pieces.shape[2]
    buffer = (
        jnp.zeros((devices_all * SLOT, piece_rows, piece_cols), jnp.float32)
        .at[slot_index]
        .set(pieces)
    )
    shaped = buffer.reshape(row_devices, col_devices, SLOT, piece_rows, piece_cols)
    arrived = joined_exchange(
        shaped.astype(jnp.bfloat16), ("row", "col"), ("row", "col"), (0, 1), (0, 1)
    ).astype(shaped.dtype)
    moved_pieces = arrived.reshape(devices_all * SLOT, piece_rows, piece_cols)
    return (upper_rows, ainv_diag, moved_pieces)


def solution(mesh):
    in_specs = (
        P("row", "col"),
        P("col", "row"),
        P("col", "row"),
        P(),
        P(("row", "col"), None, None),
        P(("row", "col"), None),
    )
    out_specs = (P("col", "row"), P("col", "row"), P(("row", "col"), None, None))
    return jax.shard_map(local, mesh=mesh, in_specs=in_specs, out_specs=out_specs, check_vma=False)
```

profile of v0, /device:TPU:1, one launch (start us, length us, event | category | flops | bytes accessed | tf_op | source)
XLA Modules:
  0.0 332.0 jit_solution(8603867656916050667)
XLA Ops:
  7.2 0.0 all-gather.2.cloned.1.call-start
  7.2 0.8 compare_bitcast_fusion
  8.0 0.1 broadcast_bitcast_fusion
  8.1 1.9 broadcast_select_fusion
  10.0 0.0 all-gather.2.cloned.1.call-update
  10.0 0.0 all-reduce.3.cloned.1.call-start
  10.1 79.1 %all-gather.2.cloned.1.call-done = bf16[1536,3072]{1,0:T(8,128)(2,1)} async-done(((bf16[96,3072]{1,0:T(8,128)(2,1)}), bf16[1536,3072]{1,0:T(8,128)(2,1)}) %all-gather.2.cloned.1.call-update) | async-done | bytes 9437200 | tf_op jit(solution)/shard_map/all_gather | solution.py:62
  89.2 5.3 %dynamic-slice_select_fusion = bf16[1536,1536]{1,0:T(8,128)(2,1)} fusion(bf16[1536,3072]{1,0:T(8,128)(2,1)} %all-gather.2.cloned.1.call-done, s32[]{:T(128)S(6)} %select_n.53, pred[]{:T(512)S(6)} %eq.27), kind=kLoop, calls=%fused_computation.4 | loop fusion | flops 2359296 | bytes 9437189 | tf_op jit(solution)/shard_map/jit(_where)/select_n | solution.py:13
  94.5 0.0 all-reduce.3.cloned.1.call-update
  94.5 0.0 reduce-scatter.2.cloned.1.call-start
  94.6 72.9 %all-reduce.3.cloned.1.call-done = bf16[1536,1536]{1,0:T(8,128)(2,1)} async-done(((bf16[1536,1536]{1,0:T(8,128)(2,1)}), bf16[1536,1536]{1,0:T(8,128)(2,1)}) %all-reduce.3.cloned.1.call-update) | async-done | bytes 4718608 | tf_op jit(solution)/shard_map/psum | solution.py:13
  167.5 20.3 %convolution_convert_fusion = bf16[1536,3072]{1,0:T(8,128)(2,1)} fusion(bf16[1536,1536]{1,0:T(8,128)(2,1)} %all-reduce.3.cloned.1.call-done, bf16[3072,1536]{1,0:T(8,128)(2,1)} %param.6), kind=kOutput, calls=%fused_computation.1 | convolution fusion | flops 14500233216 | bytes 23592960 | tf_op jit(solution)/shard_map/dot_general | solution.py:67
  187.8 0.0 copy-start.3
  187.8 0.0 reduce-scatter.2.cloned.1.call-update
  187.8 0.0 copy-start
  187.8 0.6 copy-done.3
  188.5 0.1 iota_compare_fusion
  188.6 0.1 fusion.5
  188.8 0.2 fusion.8
  189.0 3.5 %broadcast_in_dim.39 = f32[384,32,128]{2,1,0:T(8,128)} broadcast(f32[]{:T(128)} %constant.65.clone.1), dimensions={} | broadcast | bytes 6291460 | tf_op jit(solution)/shard_map/broadcast_in_dim | solution.py:92
  192.5 0.0 copy-done
  192.5 23.5 %scatter_fusion = f32[384,32,128]{2,1,0:T(8,128)} fusion(f32[384,32,128]{2,1,0:T(8,128)} %broadcast_in_dim.39, s32[192]{0:T(256)S(1)} %bitcast.46, f32[192,32,128]{2,1,0:T(8,128)S(1)} %copy-done), kind=kCustom, calls=%fused_computation | custom fusion | bytes 9437952 | tf_op jit(solution)/shard_map/scatter | solution.py:94
  216.0 5.3 %convert_element_type.54 = bf16[384,32,128]{2,1,0:T(8,128)(2,1)} convert(f32[384,32,128]{2,1,0:T(8,128)} %scatter_fusion) | non-fusion elementwise | flops 1572864 | bytes 9437184 | tf_op jit(solution)/shard_map/convert_element_type | solution.py:98
  221.3 9.8 %all-to-all-start.1 = ((bf16[128,1,1,3,32,128]{5,4,3,2,1,0:T(8,128)(2,1)}), bf16[128,1,1,3,32,128]{5,4,3,2,1,0:T(8,128)(2,1)S(1)}, u32[]{:S(2)}, u32[]{:S(2)}) async-start(bf16[128,1,1,3,32,128]{5,4,3,2,1,0:T(8,128)(2,1)} %bitcast.38), calls=%async_computation.2 | async-start | bytes 6291456 | tf_op jit(solution)/shard_map/all_to_all | solution.py:39
  231.2 74.3 %reduce-scatter.2.cloned.1.call-done = bf16[96,3072]{1,0:T(8,128)(2,1)} async-done(((bf16[1536,3072]{1,0:T(8,128)(2,1)}), bf16[96,3072]{1,0:T(8,128)(2,1)}) %reduce-scatter.2.cloned.1.call-update) | async-done | bytes 589840 | tf_op jit(solution)/shard_map/reduce_scatter | solution.py:66
  305.5 1.2 select_convert_fusion
  306.7 0.0 copy-start.1
  306.7 0.8 copy-done.1
  307.5 3.9 %fusion.2 = bf16[96,768]{1,0:T(8,128)(2,1)S(1)} fusion(bf16[96,3072]{1,0:T(8,128)(2,1)S(1)} %select_convert_fusion, bf16[1536,3072]{1,0:T(8,128)(2,1)} %all-gather.2.cloned.1.call-done, s32[]{:T(128)S(6)} %select_n.56), kind=kOutput, calls=%fused_computation.7 | convolution fusion | flops 453058560 | bytes 5455876 | tf_op jit(solution)/shard_map/dot_general | solution.py:76
  311.5 0.2 reshape.62
  311.7 0.7 copy.18
  312.4 0.0 all-to-all-done.1
  312.4 6.5 %all-to-all-start = ((bf16[8,96,96]{2,1,0:T(8,128)(2,1)}), bf16[8,96,96]{2,1,0:T(8,128)(2,1)S(1)}, u32[]{:S(2)}, u32[]{:S(2)}) async-start(bf16[8,96,96]{2,1,0:T(8,128)(2,1)} %bitcast.34), calls=%async_computation.1 | async-start | bytes 393216 | tf_op jit(solution)/shard_map/all_to_all | solution.py:23
  318.9 0.0 copy-start.2
  318.9 3.8 %bitcast_convert_fusion = f32[384,32,128]{2,1,0:T(8,128)} fusion(bf16[128,1,1,3,32,128]{5,4,3,2,1,0:T(8,128)(2,1)S(1)} %all-to-all-done.1), kind=kLoop, calls=%fused_computation.5 | loop fusion | flops 1572864 | bytes 9437184 | tf_op jit(solution)/shard_map/convert_element_type | solution.py:99
  322.7 2.1 all-to-all-done
  324.8 0.0 copy-done.2
  324.8 0.6 sub.15
  (9 shorter events, 0.1 us)
Async XLA Ops:
  7.2 82.0 %all-gather.2.cloned.1.call-start = ((), (), s32[]{:S(2)}) async-start(), calls=%async_computation.3 | async-start | bytes 10027008 | tf_op jit(solution)/shard_map/all_gather | solution.py:62
  10.0 157.4 %all-reduce.3.cloned.1.call-start = ((), (), s32[]{:S(2)}) async-start(), calls=%async_computation.4 | async-start | bytes 9437184 | tf_op jit(solution)/shard_map/psum | solution.py:13
  94.5 211.0 %reduce-scatter.2.cloned.1.call-start = ((), (), s32[]{:S(2)}) async-start(), calls=%async_computation.5 | async-start | bytes 10027008 | tf_op jit(solution)/shard_map/reduce_scatter | solution.py:66
  187.8 0.7 copy-start.3
  187.8 4.7 %copy-start = (f32[192,32,128]{2,1,0:T(8,128)S(1)}, f32[192,32,128]{2,1,0:T(8,128)}, u32[]{:S(2)}) copy-start(f32[192,32,128]{2,1,0:T(8,128)} %param.10) | copy-start | bytes 9437188
  221.3 91.1 %all-to-all-start.1 = ((bf16[128,1,1,3,32,128]{5,4,3,2,1,0:T(8,128)(2,1)}), bf16[128,1,1,3,32,128]{5,4,3,2,1,0:T(8,128)(2,1)S(1)}, u32[]{:S(2)}, u32[]{:S(2)}) async-start(bf16[128,1,1,3,32,128]{5,4,3,2,1,0:T(8,128)(2,1)} %bitcast.38), calls=%async_computation.2 | async-start | bytes 6291456 | tf_op jit(solution)/shard_map/all_to_all | solution.py:39
  306.7 0.8 copy-start.1
  312.4 12.3 %all-to-all-start = ((bf16[8,96,96]{2,1,0:T(8,128)(2,1)}), bf16[8,96,96]{2,1,0:T(8,128)(2,1)S(1)}, u32[]{:S(2)}, u32[]{:S(2)}) async-start(bf16[8,96,96]{2,1,0:T(8,128)(2,1)} %bitcast.34), calls=%async_computation.1 | async-start | bytes 393216 | tf_op jit(solution)/shard_map/all_to_all | solution.py:23
  318.9 5.9 %copy-start.2 = (f32[96,96]{1,0:T(8,128)S(1)}, f32[96,96]{1,0:T(8,128)}, u32[]{:S(2)}) copy-start(f32[96,96]{1,0:T(8,128)} %param.8) | copy-start | bytes 110596
Sparse Core Ops, SparseCore 0:
  10.7 78.4 all-gather.1
  94.6 72.7 all-reduce.2
  187.9 117.5 reduce-scatter.1
where the time goes:
time: 333 us; the launch traced here: 332 us
  waiting for transfers between devices  228 us (68%)
  local copies, waits for them, and re-layouts  29.5 us (9%)
  matrix products  24.3 us (7%)
  other arithmetic  19.5 us (6%)
  starting transfers between devices  16.4 us (5%)
  between operations  13.9 us (4%)
    all_gather x1, waiting for transfers between devices, local(): gathered = lax.all_gather(masked, 'col', axis=0, tiled=True)  79.1 us
    reduce_scatter x1, waiting for transfers between devices, local(): lax.psum_scatter(lax.dot_general(cross_rows, ainv_anc, (((1,), (1,)), (()...  74.3 us
    psum x1, waiting for transfers between devices, broadcast(): return lax.psum(jnp.where(mine, value, jnp.zeros_like(value)), axis)  72.9 us
    scatter x1, local copies, waits for them, and re-layouts, local(): buffer = jnp.zeros((devices_all * SLOT, piece_rows, piece_cols), jnp.floa...  23.5 us
    dot_general x1, matrix products, local(): lax.dot_general(cross_rows, ainv_anc, (((1,), (1,)), ((), ())), preferred...  20.3 us
    all_to_all x1, starting transfers between devices, joined_exchange(): parts = lax.all_to_all(parts, axis, split_axis=0, concat_axis=0, tiled=True)  9.85 us
  transfers between devices with their start and end apart: 5, of which 4 were waited for; matrix products, arithmetic and copies ran while one was open for 13% of the time, Pallas kernels for 0%

commit v1 on v0

--- a/solution.py
+++ b/solution.py
@@ -59,7 +59,8 @@
         jnp.broadcast_to(keep_blocks[:, :, None], (1, block_count, AB)).reshape(1, local_rows) > 0
     )
     masked = jnp.where(keep_rows, l_panel, jnp.zeros_like(l_panel))
-    gathered = lax.all_gather(masked, "col", axis=0, tiled=True)
+    copies = jnp.concatenate([masked] * lax.axis_size("col"), axis=0)
+    gathered = lax.all_to_all(copies, "col", 0, 0, tiled=True)
     offset = col_index % group_ratio * cross_width
     own_cross = lax.dynamic_slice_in_dim(gathered, offset, cross_width, 1)
     cross_rows = broadcast(own_cross, "row", col_index // group_ratio)

time: 333 us -> 416 us (1.25)
  waiting for transfers between devices: 228 us -> 290 us
  other arithmetic: 19.5 us -> 28 us
  starting transfers between devices: 16.4 us -> 24.1 us
    all_to_all x0 -> x1, waiting for transfers between devices: none -> 139 us  [local(): gathered = lax.all_to_all(copies, 'col', 0, 0, tiled=True)]
    all_gather x1 -> x0, waiting for transfers between devices: 79.1 us -> none  [local(): gathered = lax.all_gather(masked, 'col', axis=0, tiled=True)]
    unnamed x0 -> x15, other arithmetic: none -> 10.2 us
    all_to_all x0 -> x1, starting transfers between devices: none -> 7.62 us  [local(): gathered = lax.all_to_all(copies, 'col', 0, 0, tiled=True)]
  transfers between devices with their start and end apart: 5 -> 5, of which waited for: 4 -> 4; matrix products, arithmetic and copies ran while one was open for 13% -> 10% of each run, Pallas kernels for 0% -> 0%
where the time goes in v1:
time: 416 us; the launch traced here: 414 us
  waiting for transfers between devices  290 us (70%)
  local copies, waits for them, and re-layouts  33.1 us (8%)
  other arithmetic  28 us (7%)
  matrix products  24.3 us (6%)
  starting transfers between devices  24.1 us (6%)
  between operations  14.4 us (3%)
    all_to_all x1, waiting for transfers between devices, local(): gathered = lax.all_to_all(copies, 'col', 0, 0, tiled=True)  139 us
    psum x1, waiting for transfers between devices, broadcast(): return lax.psum(jnp.where(mine, value, jnp.zeros_like(value)), axis)  74.9 us
    reduce_scatter x1, waiting for transfers between devices, local(): lax.psum_scatter(lax.dot_general(cross_rows, ainv_anc, (((1,), (1,)), (()...  74.4 us
    scatter x1, local copies, waits for them, and re-layouts, local(): buffer = jnp.zeros((devices_all * SLOT, piece_rows, piece_cols), jnp.floa...  23.5 us
    dot_general x1, matrix products, local(): lax.dot_general(cross_rows, ainv_anc, (((1,), (1,)), ((), ())), preferred...  20.3 us
    unnamed x15, other arithmetic  10.2 us
    all_to_all x1, starting transfers between devices, joined_exchange(): parts = lax.all_to_all(parts, axis, split_axis=0, concat_axis=0, tiled=True)  9.89 us
  transfers between devices with their start and end apart: 5, of which 4 were waited for; matrix products, arithmetic and copies ran while one was open for 10% of the time, Pallas kernels for 0%

profile of v1, /device:TPU:1, one launch (start us, length us, event | category | flops | bytes accessed | tf_op | source)
XLA Modules:
  0.0 414.1 jit_solution(12537980777536657501)
XLA Ops:
  7.2 0.0 copy-start
  7.2 0.8 compare_bitcast_fusion
  8.0 0.1 broadcast_bitcast_fusion
  8.1 1.2 constant_dynamic-update-slice_fusion.15
  9.3 1.2 constant_dynamic-update-slice_fusion.14
  10.5 1.2 constant_dynamic-update-slice_fusion.13
  11.7 1.2 constant_dynamic-update-slice_fusion.12
  12.8 1.2 constant_dynamic-update-slice_fusion.11
  14.0 1.2 constant_dynamic-update-slice_fusion.10
  15.2 1.2 constant_dynamic-update-slice_fusion.9
  16.4 1.2 constant_dynamic-update-slice_fusion.8
  17.6 0.1 constant_dynamic-update-slice_fusion.7
  17.7 0.1 constant_dynamic-update-slice_fusion.6
  17.8 0.1 constant_dynamic-update-slice_fusion.5
  18.0 0.1 constant_dynamic-update-slice_fusion.4
  18.1 0.1 constant_dynamic-update-slice_fusion.3
  18.2 0.1 constant_dynamic-update-slice_fusion.2
  18.3 0.1 constant_dynamic-update-slice_fusion.1
  18.5 0.1 constant_dynamic-update-slice_fusion
  18.6 3.6 copy-done.1
  22.2 7.6 %all-to-all-start = ((bf16[16,96,3072]{2,1,0:T(8,128)(2,1)}), bf16[16,96,3072]{2,1,0:T(8,128)(2,1)}, u32[]{:S(2)}, u32[]{:S(2)}) async-start(bf16[16,96,3072]{2,1,0:T(8,128)(2,1)} %bitcast.41), calls=%async_computation | async-start | bytes 18874368 | tf_op jit(solution)/shard_map/all_to_all | solution.py:63
  29.9 0.0 all-reduce.3.cloned.1.call-start
  29.9 138.9 %all-to-all-done = bf16[16,96,3072]{2,1,0:T(8,128)(2,1)} async-done(((bf16[16,96,3072]{2,1,0:T(8,128)(2,1)}), bf16[16,96,3072]{2,1,0:T(8,128)(2,1)}, u32[]{:S(2)}, u32[]{:S(2)}) %all-to-all-start) | async-done | bytes 9437216 | tf_op jit(solution)/shard_map/all_to_all | solution.py:63
  168.8 5.3 %dynamic-slice_select_fusion = bf16[1536,1536]{1,0:T(8,128)(2,1)} fusion(bf16[1536,3072]{1,0:T(8,128)(2,1)} %bitcast.3, s32[]{:T(128)S(6)} %select_n.53, pred[]{:T(512)S(6)} %eq.27), kind=kLoop, calls=%fused_computation.4 | loop fusion | flops 2359296 | bytes 9437189 | tf_op jit(solution)/shard_map/jit(_where)/select_n | solution.py:13
  174.2 0.0 all-reduce.3.cloned.1.call-update
  174.2 0.0 reduce-scatter.2.cloned.1.call-start
  174.2 74.9 %all-reduce.3.cloned.1.call-done = bf16[1536,1536]{1,0:T(8,128)(2,1)} async-done(((bf16[1536,1536]{1,0:T(8,128)(2,1)}), bf16[1536,1536]{1,0:T(8,128)(2,1)}) %all-reduce.3.cloned.1.call-update) | async-done | bytes 4718608 | tf_op jit(solution)/shard_map/psum | solution.py:13
  249.1 20.3 %convolution_convert_fusion = bf16[1536,3072]{1,0:T(8,128)(2,1)} fusion(bf16[1536,1536]{1,0:T(8,128)(2,1)} %all-reduce.3.cloned.1.call-done, bf16[3072,1536]{1,0:T(8,128)(2,1)} %param.6), kind=kOutput, calls=%fused_computation.1 | convolution fusion | flops 14500233216 | bytes 23592960 | tf_op jit(solution)/shard_map/dot_general | solution.py:68
  269.4 0.0 reduce-scatter.2.cloned.1.call-update
  269.4 0.7 copy-done.5
  270.1 0.1 iota_compare_fusion
  270.2 0.1 fusion.5
  270.4 0.2 fusion.8
  270.6 3.5 broadcast_in_dim.39
  274.2 23.5 %scatter_fusion = f32[384,32,128]{2,1,0:T(8,128)} fusion(f32[384,32,128]{2,1,0:T(8,128)} %broadcast_in_dim.39, s32[192]{0:T(256)S(1)} %bitcast.49, f32[192,32,128]{2,1,0:T(8,128)S(1)} %copy-done.2), kind=kCustom, calls=%fused_computation | custom fusion | bytes 9437952 | tf_op jit(solution)/shard_map/scatter | solution.py:95
  297.6 5.3 %convert_element_type.54 = bf16[384,32,128]{2,1,0:T(8,128)(2,1)} convert(f32[384,32,128]{2,1,0:T(8,128)} %scatter_fusion) | non-fusion elementwise | flops 1572864 | bytes 9437184 | tf_op jit(solution)/shard_map/convert_element_type | solution.py:99
  302.9 9.9 %all-to-all-start.2 = ((bf16[128,1,1,3,32,128]{5,4,3,2,1,0:T(8,128)(2,1)}), bf16[128,1,1,3,32,128]{5,4,3,2,1,0:T(8,128)(2,1)S(1)}, u32[]{:S(2)}, u32[]{:S(2)}) async-start(bf16[128,1,1,3,32,128]{5,4,3,2,1,0:T(8,128)(2,1)} %bitcast.40), calls=%async_computation.3 | async-start | bytes 6291456 | tf_op jit(solution)/shard_map/all_to_all | solution.py:39
  312.9 74.4 %reduce-scatter.2.cloned.1.call-done = bf16[96,3072]{1,0:T(8,128)(2,1)} async-done(((bf16[1536,3072]{1,0:T(8,128)(2,1)}), bf16[96,3072]{1,0:T(8,128)(2,1)}) %reduce-scatter.2.cloned.1.call-update) | async-done | bytes 589840 | tf_op jit(solution)/shard_map/reduce_scatter | solution.py:67
  387.3 1.2 select_convert_fusion
  388.5 0.0 copy-start.3
  388.5 0.8 copy-done.3
  389.3 3.9 fusion.2
  393.3 0.2 reshape.64
  393.5 0.7 copy.18
  394.2 6.5 %all-to-all-start.1 = ((bf16[8,96,96]{2,1,0:T(8,128)(2,1)}), bf16[8,96,96]{2,1,0:T(8,128)(2,1)S(1)}, u32[]{:S(2)}, u32[]{:S(2)}) async-start(bf16[8,96,96]{2,1,0:T(8,128)(2,1)} %bitcast.36), calls=%async_computation.2 | async-start | bytes 393216 | tf_op jit(solution)/shard_map/all_to_all | solution.py:23
  400.8 3.8 bitcast_convert_fusion
  404.6 2.1 all-to-all-done.1
  406.7 0.6 sub.15
  (17 shorter events, 0.2 us)
Async XLA Ops:
  7.2 10.4 %copy-start = (bf16[96,3072]{1,0:T(8,128)(2,1)S(1)}, bf16[96,3072]{1,0:T(8,128)(2,1)}, u32[]{:S(2)}) copy-start(bf16[96,3072]{1,0:T(8,128)(2,1)} %param.7) | copy-start | bytes 1769476
  18.6 3.7 copy-start.1
  22.2 146.6 %all-to-all-start = ((bf16[16,96,3072]{2,1,0:T(8,128)(2,1)}), bf16[16,96,3072]{2,1,0:T(8,128)(2,1)}, u32[]{:S(2)}, u32[]{:S(2)}) async-start(bf16[16,96,3072]{2,1,0:T(8,128)(2,1)} %bitcast.41), calls=%async_computation | async-start | bytes 18874368 | tf_op jit(solution)/shard_map/all_to_all | solution.py:63
  29.9 219.2 %all-reduce.3.cloned.1.call-start = ((), (), s32[]{:S(2)}) async-start(), calls=%async_computation.4 | async-start | bytes 9437184 | tf_op jit(solution)/shard_map/psum | solution.py:13
  174.2 213.1 %reduce-scatter.2.cloned.1.call-start = ((), (), s32[]{:S(2)}) async-start(), calls=%async_computation.5 | async-start | bytes 10027008 | tf_op jit(solution)/shard_map/reduce_scatter | solution.py:67
  269.4 0.7 copy-start.5
  269.4 4.7 %copy-start.2 = (f32[192,32,128]{2,1,0:T(8,128)S(1)}, f32[192,32,128]{2,1,0:T(8,128)}, u32[]{:S(2)}) copy-start(f32[192,32,128]{2,1,0:T(8,128)} %param.10) | copy-start | bytes 9437188
  302.9 91.3 %all-to-all-start.2 = ((bf16[128,1,1,3,32,128]{5,4,3,2,1,0:T(8,128)(2,1)}), bf16[128,1,1,3,32,128]{5,4,3,2,1,0:T(8,128)(2,1)S(1)}, u32[]{:S(2)}, u32[]{:S(2)}) async-start(bf16[128,1,1,3,32,128]{5,4,3,2,1,0:T(8,128)(2,1)} %bitcast.40), calls=%async_computation.3 | async-start | bytes 6291456 | tf_op jit(solution)/shard_map/all_to_all | solution.py:39
  312.8 93.8 %copy-start.4 = (f32[96,96]{1,0:T(8,128)S(1)}, f32[96,96]{1,0:T(8,128)}, u32[]{:S(2)}) copy-start(f32[96,96]{1,0:T(8,128)} %param.8) | copy-start | bytes 110596
  388.5 0.8 copy-start.3
  394.2 12.4 %all-to-all-start.1 = ((bf16[8,96,96]{2,1,0:T(8,128)(2,1)}), bf16[8,96,96]{2,1,0:T(8,128)(2,1)S(1)}, u32[]{:S(2)}, u32[]{:S(2)}) async-start(bf16[8,96,96]{2,1,0:T(8,128)(2,1)} %bitcast.36), calls=%async_computation.2 | async-start | bytes 393216 | tf_op jit(solution)/shard_map/all_to_all | solution.py:23
Sparse Core Ops, SparseCore 0:
  174.3 74.7 all-reduce.2
  269.6 117.6 reduce-scatter.1
